TPU v7x, 32 devices: a whole 2x2x4 slice. The times are simulated.
32 devices in a mesh: slides: 2 (over y), seq: 4 (over z), sub: 4 (over x, core).
Axes of the slice: x: 2, y: 2, z: 4, core: 2. Of those that a mesh axis runs over, the one named last changes fastest.
Arguments:
- q_heads: bfloat16 [8192, 768], P(('slides', 'seq'), 'sub'), parts along dimension 0, may hold values from -8 to 8
- k_heads: bfloat16 [8192, 768], P(('slides', 'seq'), 'sub'), parts along dimension 0, may hold values from -8 to 8
- v_heads: bfloat16 [8192, 768], P(('slides', 'seq'), 'sub'), parts along dimension 0, may hold values from -6 to 6
- w_out: bfloat16 [768, 768], replicated, may hold values from -0.21875 to 0.21875
- offsets: int32 [2, 16], replicated, may hold values from 0 to 15, as said below
- valid: int32 [2], P('slides'), parts along dimension 0, may hold values from 3073 to 4096
Outputs:
- mixed: bfloat16 [8192, 768], P(('slides', 'seq'), 'sub'), parts along dimension 0
There are 2 independent parts, one for each index of `slides`. A program takes and returns all parts, laid end to end along the dimension named above; an argument that names none is the same for every part. Nothing has to cross between parts.
Inputs may be any that keep to these rules, and one draw needn't show every extreme that they name: `offsets`: row 0 lies below 4, row 1 below 16. Tiles at positions valid[0] and beyond are padding.
All inputs are finite; a program needn't handle non-finite values.
Results may differ from a plain program's by a relative error of at most 0.012.
Values may be sent and summed in bfloat16 or wider, within the bound.
A program may use at most 64 MiB of HBM per device.

v0:
```python
import jax
import jax.numpy as jnp
from jax import lax
from jax.sharding import PartitionSpec as P

HS = 48
GROUP = 4
R1 = 4
R2 = 16
NEG_FILL = -1e30


def swapped(value, axis, stride):
    mask = 2**stride
    pairs = [(source, source ^ mask) for source in range(lax.axis_size(axis))]
    return lax.ppermute(value, axis, pairs)


def pick_rows(source, stride, chosen):
    grouped = source.reshape(source.shape[0] // stride, stride, source.shape[1], source.shape[2])
    onehot = jnp.arange(stride, dtype=jnp.int32)[:, None] == chosen[None, :]
    return jnp.sum(
        jnp.where(onehot[None, :, :, None], grouped, jnp.zeros((), source.dtype)), axis=1
    )


def spread_back(maxima, totals, numer, stride, chosen):
    onehot = (jnp.arange(stride, dtype=jnp.int32)[:, None] == chosen[None, :])[None]
    count = maxima.shape[0] * stride
    full_max = jnp.where(onehot, maxima[:, None, :], NEG_FILL).reshape(count, maxima.shape[1])
    full_tot = jnp.where(onehot, totals[:, None, :], 0.0).reshape(count, maxima.shape[1])
    full_num = jnp.where(onehot[..., None], numer[:, None, :, :], 0.0).reshape(
        count, numer.shape[1], numer.shape[2]
    )
    return (full_max, full_tot, full_num)


def block_stats(q_sel, k_sel, v_sel, live):
    n_query = q_sel.shape[0]
    width = min(512, n_query)
    live_rows = live.T[:, None, :]

    def attend(q_blk):
        scores = jnp.einsum(
            "qhd,khd->hqk", q_blk, k_sel, preferred_element_type=jnp.float32
        ) * HS ** (-0.5)
        scores = jnp.where(live_rows, scores, NEG_FILL)
        peak = jnp.max(scores, axis=2)
        probs = jnp.exp(scores - peak[:, :, None])
        mass = jnp.sum(probs, axis=2)
        weighted = jnp.einsum(
            "hqk,khd->qhd", probs.astype(jnp.bfloat16), v_sel, preferred_element_type=jnp.float32
        )
        return (peak.T, mass.T, weighted)

    peak, mass, weighted = lax.map(
        attend, q_sel.reshape(n_query // width, width, q_sel.shape[1], q_sel.shape[2])
    )
    return (
        peak.reshape(n_query, q_sel.shape[1]),
        mass.reshape(n_query, q_sel.shape[1]),
        weighted.reshape(n_query, q_sel.shape[1], q_sel.shape[2]),
    )


def local(q_heads, k_heads, v_heads, w_out, offsets, valid):
    tok_rows = q_heads.shape[0]
    head_cols = q_heads.shape[1]
    local_heads = head_cols // HS
    seq_index = lax.axis_index("seq")
    sub_index = lax.axis_index("sub")
    block_start = seq_index * tok_rows
    mine = lax.dynamic_slice_in_dim(offsets, sub_index * local_heads, local_heads, 1)
    limit = valid[0]
    queries = q_heads.reshape(tok_rows, local_heads, HS)
    keys_local = k_heads.reshape(tok_rows, local_heads, HS)
    values_local = v_heads.reshape(tok_rows, local_heads, HS)
    own_rows = jnp.arange(tok_rows, dtype=jnp.int32)
    live_near = jnp.broadcast_to((block_start + own_rows < limit)[:, None], (tok_rows, local_heads))
    near = block_stats(queries, keys_local, values_local, live_near)
    middle_offs = mine[0]
    middle_rows = tok_rows // R1
    q_middle = pick_rows(queries, R1, middle_offs)
    kv_middle = jnp.concatenate(
        [
            pick_rows(keys_local, R1, middle_offs).reshape(middle_rows, head_cols),
            pick_rows(values_local, R1, middle_offs).reshape(middle_rows, head_cols),
        ],
        axis=1,
    )
    block_ids = seq_index.reshape(1)
    for bit_index in range(GROUP.bit_length() - 1):
        partner = swapped(kv_middle, "seq", bit_index)
        kv_middle = jnp.concatenate([kv_middle, partner], axis=0)
        block_ids = jnp.concatenate([block_ids, block_ids ^ 1 << bit_index])
    middle_pos = (
        block_ids[:, None] * tok_rows + jnp.arange(middle_rows, dtype=jnp.int32)[None, :] * R1
    )
    live_middle = middle_pos.reshape(-1, 1) + middle_offs[None, :] < limit
    middle_count = kv_middle.shape[0]
    middle = block_stats(
        q_middle,
        kv_middle[:, :head_cols].reshape(middle_count, local_heads, HS),
        kv_middle[:, head_cols:].reshape(middle_count, local_heads, HS),
        live_middle,
    )
    middle = spread_back(middle[0], middle[1], middle[2], R1, middle_offs)
    wide_offs = mine[1]
    wide_rows = tok_rows // R2
    q_wide = pick_rows(queries, R2, wide_offs)
    kv_wide = jnp.concatenate(
        [
            pick_rows(keys_local, R2, wide_offs).reshape(wide_rows, head_cols),
            pick_rows(values_local, R2, wide_offs).reshape(wide_rows, head_cols),
        ],
        axis=1,
    )
    piece = lax.all_gather(kv_wide, "seq", axis=0, tiled=True)
    run_peak = jnp.full((wide_rows, local_heads), NEG_FILL, jnp.float32)
    piece_len = piece.shape[0]
    global_row = jnp.arange(piece_len, dtype=jnp.int32)
    position = global_row // wide_rows * tok_rows + global_row % wide_rows * R2
    live_piece = position[:, None] + wide_offs[None, :] < limit
    piece_peak, piece_mass, piece_num = block_stats(
        q_wide,
        piece[:, :head_cols].reshape(piece_len, local_heads, HS),
        piece[:, head_cols:].reshape(piece_len, local_heads, HS),
        live_piece,
    )
    new_peak = jnp.maximum(run_peak, piece_peak)
    new_scale = jnp.exp(piece_peak - new_peak)
    wide = (new_peak, new_scale * piece_mass, new_scale[..., None] * piece_num)
    wide = spread_back(wide[0], wide[1], wide[2], R2, wide_offs)
    top = jnp.maximum(jnp.maximum(near[0], middle[0]), wide[0])
    denom = jnp.zeros_like(top)
    numer = jnp.zeros_like(near[2])
    for peak, mass, partial_num in (near, middle, wide):
        weight = jnp.exp(peak - top)
        denom = denom + weight * mass
        numer = numer + weight[..., None] * partial_num
    attn = (numer / denom[..., None]).reshape(tok_rows, head_cols).astype(jnp.bfloat16)
    w_cols = lax.dynamic_slice_in_dim(w_out, sub_index * head_cols, head_cols, 1)
    projected = jnp.dot(
        lax.all_gather(attn, "sub", axis=1, tiled=True), w_cols, preferred_element_type=jnp.float32
    )
    keep = block_start + own_rows < limit
    return jnp.where(keep[:, None], projected, 0.0).astype(jnp.bfloat16)


def solution(mesh):
    placed = (
        P(("slides", "seq"), "sub"),
        P(("slides", "seq"), "sub"),
        P(("slides", "seq"), "sub"),
        P(),
        P(),
        P("slides"),
    )
    return jax.shard_map(
        local, mesh=mesh, in_specs=placed, out_specs=P(("slides", "seq"), "sub"), check_vma=False
    )
```

profile of v0, /device:TPU:0, one launch (start us, length us, event | category | flops | bytes accessed | tf_op | source)
XLA Modules:
  0.0 160.5 jit_solution(14482707209866753938)
XLA Ops:
  6.5 1.3 copy.46
  7.8 0.8 constant_dynamic-slice_fusion
  8.6 1.2 copy.47
  9.8 1.2 copy.49
  11.0 1.5 reshape_reshape.22
  12.5 1.5 reshape_reshape.23
  14.1 1.5 reshape_reshape.24
  15.6 6.2 %select_reduce_fusion.5 = (bf16[256,4,48]{2,1,0:T(4,128)(2,1)}, bf16[256,4,48]{2,1,0:T(4,128)(2,1)}, bf16[256,4,48]{2,1,0:T(4,128)(2,1)}) fusion(bf16[256,4,4,48]{3,2,1,0:T(4,128)(2,1)} %reshape_reshape.22, pred[4,4]{1,0:T(4,128)(4,1)S(1)} %iota_compare_fusion.1, bf16[256,4,4,48]{3,2,1,0:T(4,128)(2,1)} %reshape_reshape.23, ...), kind=kLoop, calls=%fused_computation.36 | loop fusion | flops 1032192 | bytes 1474576 | tf_op jit(solution)/shard_map/reduce_sum | solution.py:22
  21.8 1.8 %copy.50 = bf16[256,4,48]{0,2,1:T(8,128)(2,1)} copy(bf16[256,4,48]{2,1,0:T(4,128)(2,1)} %get-tuple-element.148) | data formatting | bytes 196608 | tf_op jit(solution)/shard_map/reduce_sum | solution.py:22
  23.6 1.7 %copy.48 = bf16[256,4,48]{0,2,1:T(8,128)(2,1)} copy(bf16[256,4,48]{2,1,0:T(4,128)(2,1)} %get-tuple-element.147) | data formatting | bytes 196608 | tf_op jit(solution)/shard_map/reduce_sum | solution.py:22
  25.4 1.6 %pad_maximum_fusion.2 = bf16[256,384]{0,1:T(8,128)(2,1)} fusion(bf16[256,192]{0,1:T(8,128)(2,1)} %bitcast.123, bf16[256,192]{0,1:T(8,128)(2,1)} %bitcast.126), kind=kLoop, calls=%fused_computation.52 | loop fusion | flops 393216 | bytes 393216 | tf_op jit(solution)/shard_map/concatenate | solution.py:84
  27.0 3.1 %collective-permute-start = (bf16[256,384]{0,1:T(8,128)(2,1)}, bf16[256,384]{0,1:T(8,128)(2,1)}, u32[]{:S(2)}, u32[]{:S(2)}) collective-permute-start(bf16[256,384]{0,1:T(8,128)(2,1)} %pad_maximum_fusion.2), channel_id=1, source_target_pairs={{0,4},{4,0},{8,12},{12,8},{1,5},{5,1},{9,13},{13,9},{2,6},{6,2},{1... | collective-permute-start | bytes 589832 | tf_op jit(solution)/shard_map/ppermute | solution.py:16
  30.0 1.0 reshape_reshape.21
  31.1 1.5 reshape_reshape.25
  32.6 1.5 reshape_reshape.26
  34.1 1.5 reshape_reshape.27
  35.6 0.1 copy.45
  36.5 28.2 %while.3 = (s32[]{:T(128)}, f32[2,512,4]{1,2,0:T(4,128)}, f32[2,512,4]{1,2,0:T(4,128)}, f32[2,512,4,48]{1,0,3,2:T(2,128)}, bf16[2,512,4,48]{1,3,2,0:T(8,128)(2,1...) while((s32[]{:T(128)}, f32[2,512,4]{1,2,0:T(4,128)}, ...), condition=%wide.region_3.4_spmd.clone, body=%wide.region_0.3_spmd.clone.sunk | while | flops 425717760 | bytes 30018820 | solution.py:56
  36.7 1.5 fusion.68
  38.2 2.1 %fusion.69 = f32[4,512]{1,0:T(4,128)S(1)} fusion(f32[4,512,1024]{2,1,0:T(8,128)S(1)} %get-tuple-element.239, f32[4,512]{1,0:T(4,128)S(1)} %get-tuple-element.240, pred[1024]{0:T(1024)(128)(4,1)S(1)} %get-tuple-element.270), kind=kLoop, calls=%fused_computation.5.clone.1 | loop fusion | flops 8386560 | bytes 8406016 | tf_op jit(solution)/shard_map/while/body/eval_jaxpr/reduce_sum | solution.py:50
  40.3 1.8 %fusion.70 = f32[1,512,4,48]{1,3,2,0:T(8,128)S(1)} fusion(bf16[1024,4,48]{0,2,1:T(8,128)(2,1)S(1)} %copy-done.10, f32[4,512,1024]{2,1,0:T(8,128)S(1)} %get-tuple-element.239, f32[4,512]{1,0:T(4,128)S(1)} %get-tuple-element.240, pred[1024]{0:T(1024)(128)(4,1)S(1)} %get-tuple-element.270), kind=kOutput, calls=%fused_computation.8.clone.1 | convolution fusion | flops 209715200 | bytes 9184256 | tf_op jit(solution)/shard_map/while/body/eval_jaxpr/hqk,khd->qhd/dot_general | solution.py:51
  42.2 0.4 copy.83
  42.6 8.1 %dynamic_update_slice.35 = f32[2,512,4,48]{1,0,3,2:T(2,128)} dynamic-update-slice(f32[2,512,4,48]{1,0,3,2:T(2,128)} %get-tuple-element.256, f32[1,512,4,48]{1,0,3,2:T(1,128)S(1)} %copy.83, s32[]{:T(128)S(6)} %copy.91, s32[]{:T(128)} %constant.119.clone.1..sunk, s32[]{:T(128)} %constant.119.clone.1..sunk, s32[]{:T(128)} %constant.119.clone.1..sunk) | dynamic-update-slice | bytes 786436 | tf_op jit(solution)/shard_map/while/body/jit(dynamic_update_index_in_dim)/dynamic_update_slice | solution.py:56
  50.7 1.5 fusion.68
  52.2 2.1 %fusion.69 = f32[4,512]{1,0:T(4,128)S(1)} fusion(f32[4,512,1024]{2,1,0:T(8,128)S(1)} %get-tuple-element.239, f32[4,512]{1,0:T(4,128)S(1)} %get-tuple-element.240, pred[1024]{0:T(1024)(128)(4,1)S(1)} %get-tuple-element.270), kind=kLoop, calls=%fused_computation.5.clone.1 | loop fusion | flops 8386560 | bytes 8406016 | tf_op jit(solution)/shard_map/while/body/eval_jaxpr/reduce_sum | solution.py:50
  54.4 1.8 %fusion.70 = f32[1,512,4,48]{1,3,2,0:T(8,128)S(1)} fusion(bf16[1024,4,48]{0,2,1:T(8,128)(2,1)S(1)} %copy-done.10, f32[4,512,1024]{2,1,0:T(8,128)S(1)} %get-tuple-element.239, f32[4,512]{1,0:T(4,128)S(1)} %get-tuple-element.240, pred[1024]{0:T(1024)(128)(4,1)S(1)} %get-tuple-element.270), kind=kOutput, calls=%fused_computation.8.clone.1 | convolution fusion | flops 209715200 | bytes 9184256 | tf_op jit(solution)/shard_map/while/body/eval_jaxpr/hqk,khd->qhd/dot_general | solution.py:51
  56.2 0.4 copy.83
  56.6 8.1 %dynamic_update_slice.35 = f32[2,512,4,48]{1,0,3,2:T(2,128)} dynamic-update-slice(f32[2,512,4,48]{1,0,3,2:T(2,128)} %get-tuple-element.256, f32[1,512,4,48]{1,0,3,2:T(1,128)S(1)} %copy.83, s32[]{:T(128)S(6)} %copy.91, s32[]{:T(128)} %constant.119.clone.1..sunk, s32[]{:T(128)} %constant.119.clone.1..sunk, s32[]{:T(128)} %constant.119.clone.1..sunk) | dynamic-update-slice | bytes 786436 | tf_op jit(solution)/shard_map/while/body/jit(dynamic_update_index_in_dim)/dynamic_update_slice | solution.py:56
  64.7 2.2 %copy.73 = f32[24,8,2,512]{3,1,2,0:T(8,128)} copy(f32[24,8,2,512]{3,2,1,0:T(2,128)} %bitcast.129) | data formatting | bytes 1572864
  67.0 4.9 %select_reduce_fusion.2 = (bf16[64,4,48]{2,1,0:T(4,128)(2,1)S(1)}, bf16[64,4,48]{2,1,0:T(4,128)(2,1)S(1)}, bf16[64,4,48]{2,1,0:T(4,128)(2,1)S(1)}) fusion(bf16[64,16,4,48]{3,2,1,0:T(4,128)(2,1)S(1)} %copy-done.2, pred[16,4]{1,0:T(8,128)(4,1)S(1)} %iota_compare_fusion, bf16[64,16,4,48]{3,2,1,0:T(4,128)(2,1)} %reshape_reshape.26, ...), kind=kLoop, calls=%fused_computation.33 | loop fusion | flops 1142784 | bytes 1253440 | tf_op jit(solution)/shard_map/reduce_sum | solution.py:22
  71.9 0.1 copy.57
  72.0 0.1 copy.55
  72.2 14.0 %all_gather.6 = bf16[256,384]{1,0:T(8,128)(2,1)S(1)} all-gather(bf16[64,384]{1,0:T(8,128)(2,1)S(1)} %copy.58), channel_id=1, replica_groups=mesh['slides'=2,'seq'=4,'sub'=4] {'seq'}, dimensions={0}, use_global_device_ids=true | all-gather | bytes 245760 | tf_op jit(solution)/shard_map/all_gather | solution.py:118
  86.3 0.1 fusion.50
  86.7 0.2 fusion.51
  86.9 0.2 fusion.35
  87.1 0.3 fusion.28
  87.4 0.8 copy.65
  88.1 1.2 broadcast_in_dim.317
  89.3 1.9 %broadcast_in_dim.318 = f32[1024,192]{1,0:T(8,128)} reshape(f32[64,16,4,48]{3,2,1,0:T(4,128)S(1)} %broadcast_in_dim.317) | data formatting | bytes 1572864 | tf_op jit(solution)/shard_map/jit(_where)/broadcast_in_dim | solution.py:32
  91.2 2.5 %copy.66 = f32[1024,192]{0,1:T(8,128)} copy(f32[1024,192]{1,0:T(8,128)} %broadcast_in_dim.318) | data formatting | bytes 1572864 | tf_op jit(solution)/shard_map/jit(_where)/broadcast_in_dim | solution.py:32
  93.9 1.0 pad_maximum_fusion.1
  94.9 0.7 collective-permute-start.1
  95.6 0.1 broadcast_in_dim.302
  95.9 0.7 broadcast_in_dim.323
  96.6 0.3 broadcast_in_dim.293
  97.1 0.7 broadcast_in_dim.309
  97.9 13.9 %collective-permute-done.1 = bf16[512,384]{0,1:T(8,128)(2,1)S(1)} collective-permute-done((bf16[512,384]{0,1:T(8,128)(2,1)S(1)}, bf16[512,384]{0,1:T(8,128)(2,1)S(1)}, u32[]{:S(2)}, u32[]{:S(2)}) %collective-permute-start.1) | collective-permute-done | bytes 393248 | tf_op jit(solution)/shard_map/ppermute | solution.py:16
  111.8 1.0 pad_maximum_fusion
  112.9 0.8 fusion.17
  113.7 1.7 %fusion.18 = f32[4,256]{1,0:T(4,128)} fusion(f32[4,256,1024]{2,1,0:T(8,128)S(1)} %get-tuple-element.185, f32[4,256]{1,0:T(4,128)S(1)} %get-tuple-element.184, pred[4,1024]{1,0:T(4,128)(4,1)S(1)} %add_compare_fusion), kind=kLoop, calls=%fused_computation.20 | loop fusion | flops 4193280 | bytes 4206592 | tf_op jit(solution)/shard_map/while/body/eval_jaxpr/reduce_sum | solution.py:50
  115.4 1.2 fusion.25
  116.6 1.0 copy.62
  117.6 1.3 broadcast_in_dim.312
  118.9 1.9 %broadcast_in_dim.313 = f32[1024,192]{1,0:T(8,128)} reshape(f32[256,4,4,48]{3,2,1,0:T(4,128)S(1)} %broadcast_in_dim.312) | data formatting | bytes 1572864 | tf_op jit(solution)/shard_map/jit(_where)/broadcast_in_dim | solution.py:32
  120.8 1.7 %copy.63 = f32[1024,192]{0,1:T(8,128)S(1)} copy(f32[1024,192]{1,0:T(8,128)} %broadcast_in_dim.313) | data formatting | bytes 1572864 | tf_op jit(solution)/shard_map/jit(_where)/broadcast_in_dim | solution.py:32
  122.5 1.7 %broadcast_in_dim.319 = f32[256,4,4]{1,0,2:T(8,128)} broadcast(f32[256,4]{0,1:T(4,128)} %bitcast.137), dimensions={0,2} | broadcast | bytes 20480 | tf_op jit(solution)/shard_map/jit(_where)/broadcast_in_dim | solution.py:31
  124.1 1.9 %broadcast_in_dim.320 = f32[1024,4]{0,1:T(4,128)} reshape(f32[256,4,4]{1,0,2:T(8,128)} %broadcast_in_dim.319) | data formatting | bytes 32768 | tf_op jit(solution)/shard_map/jit(_where)/broadcast_in_dim | solution.py:31
  126.1 1.0 broadcast_in_dim.298
  127.0 1.9 %broadcast_in_dim.299 = f32[1024,4]{0,1:T(4,128)} reshape(f32[256,4,4]{1,0,2:T(8,128)} %broadcast_in_dim.298) | data formatting | bytes 32768 | tf_op jit(solution)/shard_map/jit(_where)/broadcast_in_dim | solution.py:30
  129.0 0.8 multiply_add_fusion
  129.8 1.1 fusion.29
  130.9 19.9 %all-gather.2.cloned.1.call-done = bf16[1024,768]{0,1:T(8,128)(2,1)} async-done(((bf16[1024,192]{0,1:T(8,128)(2,1)}), bf16[1024,768]{0,1:T(8,128)(2,1)}) %all-gather.2.cloned.1.call-update) | async-done | bytes 1572880 | tf_op jit(solution)/shard_map/all_gather | solution.py:144
  150.8 2.9 %fusion.23 = bf16[1024,192]{0,1:T(8,128)(2,1)} fusion(bf16[1024,768]{0,1:T(8,128)(2,1)} %all-gather.2.cloned.1.call-done, bf16[768,768]{1,0:T(8,128)(2,1)S(1)} %copy-done, s32[]{:T(128)S(6)} %select_n.145, pred[1024]{0:T(1024)(128)(4,1)S(1)} %get-tuple-element.278), kind=kOutput, calls=%fused_computation.25 | convolution fusion | flops 302383104 | bytes 2360324 | tf_op jit(solution)/shard_map/dot_general | solution.py:143
  (80 shorter events, 1.3 us)
Async XLA Ops:
  6.5 144.3 %copy-start = (bf16[768,768]{1,0:T(8,128)(2,1)S(1)}, bf16[768,768]{1,0:T(8,128)(2,1)}, u32[]{:S(2)}) copy-start(bf16[768,768]{1,0:T(8,128)(2,1)} %param.11) | copy-start | bytes 3538948
  6.5 144.3 %all-gather.2.cloned.1.call-start = ((), (), s32[]{:S(2)}) async-start(), calls=%async_computation | async-start | bytes 1966080 | tf_op jit(solution)/shard_map/all_gather | solution.py:144
  8.6 13.2 %copy-start.15 = (s32[4]{0:T(128)}, s32[4]{0:T(128)S(1)}, u32[]{:S(2)}) copy-start(s32[4]{0:T(128)S(1)} %get-tuple-element.180) | copy-start | bytes 52
  12.5 17.5 %copy-start.5 = (bf16[1024,192]{0,1:T(8,128)(2,1)S(1)}, bf16[1024,192]{0,1:T(8,128)(2,1)}, u32[]{:S(2)}) copy-start(bf16[1024,192]{0,1:T(8,128)(2,1)} %param.8) | copy-start | bytes 1179652
  12.5 3.1 %copy-start.17 = (pred[4,4]{1,0:T(4,128)(4,1)}, pred[4,4]{1,0:T(4,128)(4,1)S(1)}, u32[]{:S(2)}) copy-start(pred[4,4]{1,0:T(4,128)(4,1)S(1)} %iota_compare_fusion.1) | copy-start | bytes 52
  21.8 14.6 %copy-start.1 = (bf16[1024,192]{0,1:T(8,128)(2,1)S(1)}, bf16[1024,192]{0,1:T(8,128)(2,1)}, u32[]{:S(2)}) copy-start(bf16[1024,192]{0,1:T(8,128)(2,1)} %param.9) | copy-start | bytes 1179652
  21.8 13.8 %copy-start.18 = (pred[4,4]{1,0:T(4,128)(4,1)S(1)}, pred[4,4]{1,0:T(4,128)(4,1)}, u32[]{:S(2)}) copy-start(pred[4,4]{1,0:T(4,128)(4,1)} %copy-done.17) | copy-start | bytes 52
  27.0 66.9 %collective-permute-start = (bf16[256,384]{0,1:T(8,128)(2,1)}, bf16[256,384]{0,1:T(8,128)(2,1)}, u32[]{:S(2)}, u32[]{:S(2)}) collective-permute-start(bf16[256,384]{0,1:T(8,128)(2,1)} %pad_maximum_fusion.2), channel_id=1, source_target_pairs={{0,4},{4,0},{8,12},{12,8},{1,5},{5,1},{9,13},{13,9},{2,6},{6,2},{1... | collective-permute-start | bytes 589832 | tf_op jit(solution)/shard_map/ppermute | solution.py:16
  31.1 4.7 %copy-start.6 = (bf16[2,512,4,48]{1,0,3,2:T(2,128)(2,1)S(1)}, bf16[2,512,4,48]{1,0,3,2:T(2,128)(2,1)}, u32[]{:S(2)}) copy-start(bf16[2,512,4,48]{1,0,3,2:T(2,128)(2,1)} %reshape_reshape.21) | copy-start | bytes 1179652
  36.5 30.5 %copy-start.2 = (bf16[64,16,4,48]{3,2,1,0:T(4,128)(2,1)S(1)}, bf16[64,16,4,48]{3,2,1,0:T(4,128)(2,1)}, u32[]{:S(2)}) copy-start(bf16[64,16,4,48]{3,2,1,0:T(4,128)(2,1)} %reshape_reshape.25) | copy-start | bytes 1179652
  38.2 2.1 %copy-start.11 = (f32[2,512,4]{1,2,0:T(4,128)S(1)}, f32[2,512,4]{1,2,0:T(4,128)}, u32[]{:S(2)}) copy-start(f32[2,512,4]{1,2,0:T(4,128)} %get-tuple-element.254) | copy-start | bytes 49156 | tf_op jit(solution)/shard_map/while
  38.2 2.1 %copy-start.13 = (f32[2,512,4]{1,2,0:T(4,128)S(1)}, f32[2,512,4]{1,2,0:T(4,128)}, u32[]{:S(2)}) copy-start(f32[2,512,4]{1,2,0:T(4,128)} %get-tuple-element.255) | copy-start | bytes 49156 | tf_op jit(solution)/shard_map/while
  38.2 2.2 %copy-start.10 = (bf16[1024,4,48]{0,2,1:T(8,128)(2,1)S(1)}, bf16[1024,4,48]{0,2,1:T(8,128)(2,1)}, u32[]{:S(2)}) copy-start(bf16[1024,4,48]{0,2,1:T(8,128)(2,1)} %get-tuple-element.269) | copy-start | bytes 1179652 | tf_op jit(solution)/shard_map/while
  40.3 1.9 %copy-start.12 = (f32[2,512,4]{1,2,0:T(4,128)}, f32[2,512,4]{1,2,0:T(4,128)S(1)}, u32[]{:S(2)}) copy-start(f32[2,512,4]{1,2,0:T(4,128)S(1)} %get-tuple-element.264) | copy-start | bytes 49156 | tf_op jit(solution)/shard_map/while
  40.3 1.9 %copy-start.14 = (f32[2,512,4]{1,2,0:T(4,128)}, f32[2,512,4]{1,2,0:T(4,128)S(1)}, u32[]{:S(2)}) copy-start(f32[2,512,4]{1,2,0:T(4,128)S(1)} %get-tuple-element.265) | copy-start | bytes 49156 | tf_op jit(solution)/shard_map/while
  52.2 2.1 %copy-start.11 = (f32[2,512,4]{1,2,0:T(4,128)S(1)}, f32[2,512,4]{1,2,0:T(4,128)}, u32[]{:S(2)}) copy-start(f32[2,512,4]{1,2,0:T(4,128)} %get-tuple-element.254) | copy-start | bytes 49156 | tf_op jit(solution)/shard_map/while
  52.2 2.1 %copy-start.13 = (f32[2,512,4]{1,2,0:T(4,128)S(1)}, f32[2,512,4]{1,2,0:T(4,128)}, u32[]{:S(2)}) copy-start(f32[2,512,4]{1,2,0:T(4,128)} %get-tuple-element.255) | copy-start | bytes 49156 | tf_op jit(solution)/shard_map/while
  52.2 2.2 %copy-start.10 = (bf16[1024,4,48]{0,2,1:T(8,128)(2,1)S(1)}, bf16[1024,4,48]{0,2,1:T(8,128)(2,1)}, u32[]{:S(2)}) copy-start(bf16[1024,4,48]{0,2,1:T(8,128)(2,1)} %get-tuple-element.269) | copy-start | bytes 1179652 | tf_op jit(solution)/shard_map/while
  54.3 1.9 %copy-start.12 = (f32[2,512,4]{1,2,0:T(4,128)}, f32[2,512,4]{1,2,0:T(4,128)S(1)}, u32[]{:S(2)}) copy-start(f32[2,512,4]{1,2,0:T(4,128)S(1)} %get-tuple-element.264) | copy-start | bytes 49156 | tf_op jit(solution)/shard_map/while
  54.3 1.9 %copy-start.14 = (f32[2,512,4]{1,2,0:T(4,128)}, f32[2,512,4]{1,2,0:T(4,128)S(1)}, u32[]{:S(2)}) copy-start(f32[2,512,4]{1,2,0:T(4,128)S(1)} %get-tuple-element.265) | copy-start | bytes 49156 | tf_op jit(solution)/shard_map/while
  86.9 7.0 %copy-start.7 = (bf16[256,4,48]{0,2,1:T(8,128)(2,1)S(1)}, bf16[256,4,48]{0,2,1:T(8,128)(2,1)}, u32[]{:S(2)}) copy-start(bf16[256,4,48]{0,2,1:T(8,128)(2,1)} %copy.50) | copy-start | bytes 294916
  86.9 7.0 %copy-start.8 = (bf16[256,4,48]{0,2,1:T(8,128)(2,1)S(1)}, bf16[256,4,48]{0,2,1:T(8,128)(2,1)}, u32[]{:S(2)}) copy-start(bf16[256,4,48]{0,2,1:T(8,128)(2,1)} %copy.48) | copy-start | bytes 294916
  88.1 9.7 %copy-start.16 = (s32[4]{0:T(128)S(1)}, s32[4]{0:T(128)}, u32[]{:S(2)}) copy-start(s32[4]{0:T(128)} %copy-done.15) | copy-start | bytes 52
  91.2 21.7 %copy-start.9 = (bf16[256,4,48]{2,1,0:T(4,128)(2,1)S(1)}, bf16[256,4,48]{2,1,0:T(4,128)(2,1)}, u32[]{:S(2)}) copy-start(bf16[256,4,48]{2,1,0:T(4,128)(2,1)} %get-tuple-element.146) | copy-start | bytes 294916
  94.9 16.9 %collective-permute-start.1 = (bf16[512,384]{0,1:T(8,128)(2,1)S(1)}, bf16[512,384]{0,1:T(8,128)(2,1)S(1)}, u32[]{:S(2)}, u32[]{:S(2)}) collective-permute-start(bf16[512,384]{0,1:T(8,128)(2,1)S(1)} %pad_maximum_fusion.1), channel_id=1, source_target_pairs={{0,8},{4,12},{8,0},{12,4},{1,9},{5,13},{9,1},{13,5},{2,10},{6,14},... | collective-permute-start | bytes 1179656 | tf_op jit(solution)/shard_map/ppermute | solution.py:16
  120.8 9.0 %copy-start.3 = (f32[1024,192]{0,1:T(8,128)S(1)}, f32[1024,192]{0,1:T(8,128)}, u32[]{:S(2)}) copy-start(f32[1024,192]{0,1:T(8,128)} %copy.66) | copy-start | bytes 2359300
  120.8 9.0 %copy-start.4 = (f32[24,8,2,512]{3,1,2,0:T(8,128)S(1)}, f32[24,8,2,512]{3,1,2,0:T(8,128)}, u32[]{:S(2)}) copy-start(f32[24,8,2,512]{3,1,2,0:T(8,128)} %copy.73) | copy-start | bytes 2359300
Sparse Core Ops, SparseCore 0:
  131.0 19.7 all-gather.1
where the time goes:
time: 162 us; the launch traced here: 161 us
  local copies, waits for them, and re-layouts  59.1 us (36%)
  waiting for transfers between devices  33.8 us (21%)
  other arithmetic  23.1 us (14%)
  between operations  14.3 us (9%)
  blocking collectives  14 us (9%)
  matrix products  12 us (7%)
  starting transfers between devices  3.75 us (2%)
    all_gather x1, waiting for transfers between devices, local(): lax.all_gather(attn, 'sub', axis=1, tiled=True)  19.9 us
    dynamic_update_slice x6, local copies, waits for them, and re-layouts, block_stats(): lax.map(attend, q_sel.reshape(n_query // width, width, q_sel.shape[1], q_...  17 us
    all_gather x1, blocking collectives, local(): piece = lax.all_gather(kv_wide, 'seq', axis=0, tiled=True)  14 us
    ppermute x2, waiting for transfers between devices, swapped(): return lax.ppermute(value, axis, pairs)  13.9 us
    reduce_sum x2, other arithmetic, pick_rows(): jnp.sum(jnp.where(onehot[None, :, :, None], grouped, jnp.zeros((), source...  11.1 us
    broadcast_in_dim x6, local copies, waits for them, and re-layouts, spread_back(): jnp.where(onehot[..., None], numer[:, None, :, :], 0.0)  10.4 us
    another operation x6, local copies, waits for them, and re-layouts, pick_rows(): source.reshape(source.shape[0] // stride, stride, source.shape[1], source...  9.14 us
    reduce_sum x4, other arithmetic, attend(): mass = jnp.sum(probs, axis=2)  6.02 us
  transfers between devices with their start and end apart: 3, of which 2 were waited for; matrix products, arithmetic and copies ran while one was open for 32% of the time, Pallas kernels for 0%

commit v1 on v0

--- a/solution.py
+++ b/solution.py
@@ -115,7 +115,12 @@
         ],
         axis=1,
     )
-    piece = lax.all_gather(kv_wide, "seq", axis=0, tiled=True)
+    ring = [kv_wide]
+    for hop in range(3):
+        ring.append(lax.ppermute(ring[-1], "seq", [(dev, (dev + 1) % 4) for dev in range(4)]))
+    piece = jnp.roll(
+        jnp.concatenate(ring[::-1], axis=0), (lax.axis_index("seq") + 1) * ring[0].shape[0], axis=0
+    )
     run_peak = jnp.full((wide_rows, local_heads), NEG_FILL, jnp.float32)
     piece_len = piece.shape[0]
     global_row = jnp.arange(piece_len, dtype=jnp.int32)

time: 162 us -> 142 us (0.88)
  blocking collectives: 14 us -> 0 us
  local copies, waits for them, and re-layouts: 59.1 us -> 50.2 us
  waiting for transfers between devices: 33.8 us -> 36.5 us
  starting transfers between devices: 3.75 us -> 5.37 us
    all_gather x1 -> x0, blocking collectives: 14 us -> none  [local(): piece = lax.all_gather(kv_wide, 'seq', axis=0, tiled=True)]
    ppermute x0 -> x3, waiting for transfers between devices: none -> 8.42 us  [local(): lax.ppermute(ring[-1], 'seq', [(dev, (dev + 1) % 4) for dev in range(4)])]
    dynamic_update_slice x6, local copies, waits for them, and re-layouts: 17 us -> 9.32 us  [block_stats(): lax.map(attend, q_sel.reshape(n_query // width, width, q_sel.shape[1], q_...]
    ppermute x2, waiting for transfers between devices: 13.9 us -> 9.21 us  [swapped(): return lax.ppermute(value, axis, pairs)]
    ppermute x0 -> x3, starting transfers between devices: none -> 3.79 us  [local(): lax.ppermute(ring[-1], 'seq', [(dev, (dev + 1) % 4) for dev in range(4)])]
    reduce_sum x4, local copies, waits for them, and re-layouts: 3.72 us -> 0.51 us  [pick_rows(): jnp.sum(jnp.where(onehot[None, :, :, None], grouped, jnp.zeros((), source...]
    ppermute x2, starting transfers between devices: 3.75 us -> 1.58 us  [swapped(): return lax.ppermute(value, axis, pairs)]
    while x20 -> x12, local copies, waits for them, and re-layouts: 0.05 us -> 1.78 us
  transfers between devices with their start and end apart: 3 -> 6, of which waited for: 2 -> 4; matrix products, arithmetic and copies ran while one was open for 32% -> 33% of each run, Pallas kernels for 0% -> 0%
where the time goes in v1:
time: 142 us
  local copies, waits for them, and re-layouts  50.2 us (35%)
  waiting for transfers between devices  36.5 us (26%)
  other arithmetic  23.1 us (16%)
  between operations  14.3 us (10%)
  matrix products  12 us (8%)
  starting transfers between devices  5.37 us (4%)
    all_gather x1, waiting for transfers between devices, local(): lax.all_gather(attn, 'sub', axis=1, tiled=True)  18.8 us
    reduce_sum x2, other arithmetic, pick_rows(): jnp.sum(jnp.where(onehot[None, :, :, None], grouped, jnp.zeros((), source...  11.2 us
    broadcast_in_dim x6, local copies, waits for them, and re-layouts, spread_back(): jnp.where(onehot[..., None], numer[:, None, :, :], 0.0)  10.4 us
    dynamic_update_slice x6, local copies, waits for them, and re-layouts, block_stats(): lax.map(attend, q_sel.reshape(n_query // width, width, q_sel.shape[1], q_...  9.32 us
    ppermute x2, waiting for transfers between devices, swapped(): return lax.ppermute(value, axis, pairs)  9.21 us
    another operation x6, local copies, waits for them, and re-layouts, pick_rows(): source.reshape(source.shape[0] // stride, stride, source.shape[1], source...  8.97 us
    ppermute x3, waiting for transfers between devices, local(): lax.ppermute(ring[-1], 'seq', [(dev, (dev + 1) % 4) for dev in range(4)])  8.42 us
    reduce_sum x4, other arithmetic, attend(): mass = jnp.sum(probs, axis=2)  6.04 us
  transfers between devices with their start and end apart: 6, of which 4 were waited for; matrix products, arithmetic and copies ran while one was open for 33% of the time, Pallas kernels for 0%

profile of v1, /device:TPU:0, one launch (start us, length us, event | category | flops | bytes accessed | tf_op | source)
XLA Modules:
  0.0 141.7 jit_solution(106446940967610746)
XLA Ops:
  6.5 1.3 copy.46
  7.9 1.5 %reshape_reshape.25 = bf16[64,16,4,48]{3,2,1,0:T(4,128)(2,1)} reshape(bf16[1024,192]{1,0:T(8,128)(2,1)S(1)} %copy.46) | data formatting | bytes 786432 | tf_op jit(solution)/shard_map/reshape;reshape | solution.py:20
  9.4 0.7 constant_dynamic-slice_fusion.1
  10.1 1.2 copy.47
  11.3 1.5 %reshape_reshape.26 = bf16[64,16,4,48]{3,2,1,0:T(4,128)(2,1)} reshape(bf16[1024,192]{1,0:T(8,128)(2,1)S(1)} %copy.47) | data formatting | bytes 786432 | tf_op jit(solution)/shard_map/reshape;reshape | solution.py:20
  12.8 0.2 copy.49
  13.0 1.5 %reshape_reshape.27 = bf16[64,16,4,48]{3,2,1,0:T(4,128)(2,1)} reshape(bf16[1024,192]{1,0:T(8,128)(2,1)S(1)} %copy.49) | data formatting | bytes 786432 | tf_op jit(solution)/shard_map/reshape;reshape | solution.py:20
  14.5 5.2 %select_reduce_fusion.2 = (bf16[64,4,48]{2,1,0:T(4,128)(2,1)S(1)}, bf16[64,4,48]{2,1,0:T(4,128)(2,1)S(1)}, bf16[64,4,48]{2,1,0:T(4,128)(2,1)S(1)}) fusion(bf16[64,16,4,48]{3,2,1,0:T(4,128)(2,1)} %reshape_reshape.25, pred[16,4]{1,0:T(8,128)(4,1)S(1)} %iota_compare_fusion, bf16[64,16,4,48]{3,2,1,0:T(4,128)(2,1)} %reshape_reshape.26, ...), kind=kLoop, calls=%fused_computation.33 | loop fusion | flops 1142784 | bytes 1253440 | tf_op jit(solution)/shard_map/reduce_sum | solution.py:22
  20.0 3.3 %collective-permute-start.2 = (bf16[64,384]{0,1:T(8,128)(2,1)S(1)}, bf16[64,384]{0,1:T(8,128)(2,1)}, u32[]{:S(2)}, u32[]{:S(2)}) collective-permute-start(bf16[64,384]{0,1:T(8,128)(2,1)S(1)} %pad_maximum_fusion.3), channel_id=1, source_target_pairs={{0,4},{4,8},{8,12},{12,0},{1,5},{5,9},{9,13},{13,1},{2,6},{6,10},{... | collective-permute-start | bytes 147464 | tf_op jit(solution)/shard_map/ppermute | solution.py:120
  23.3 1.5 %reshape_reshape.22 = bf16[256,4,4,48]{3,2,1,0:T(4,128)(2,1)} reshape(bf16[1024,192]{1,0:T(8,128)(2,1)S(1)} %copy.46) | data formatting | bytes 786432 | tf_op jit(solution)/shard_map/reshape;reshape | solution.py:20
  24.8 1.5 %reshape_reshape.23 = bf16[256,4,4,48]{3,2,1,0:T(4,128)(2,1)} reshape(bf16[1024,192]{1,0:T(8,128)(2,1)S(1)} %copy.47) | data formatting | bytes 786432 | tf_op jit(solution)/shard_map/reshape;reshape | solution.py:20
  26.3 1.5 %reshape_reshape.24 = bf16[256,4,4,48]{3,2,1,0:T(4,128)(2,1)} reshape(bf16[1024,192]{1,0:T(8,128)(2,1)S(1)} %copy.49) | data formatting | bytes 786432 | tf_op jit(solution)/shard_map/reshape;reshape | solution.py:20
  27.8 6.0 %select_reduce_fusion.5 = (bf16[256,4,48]{2,1,0:T(4,128)(2,1)}, bf16[256,4,48]{2,1,0:T(4,128)(2,1)S(1)}, bf16[256,4,48]{2,1,0:T(4,128)(2,1)S(1)}) fusion(bf16[256,4,4,48]{3,2,1,0:T(4,128)(2,1)} %reshape_reshape.22, pred[4,4]{1,0:T(4,128)(4,1)S(1)} %iota_compare_fusion.1, bf16[256,4,4,48]{3,2,1,0:T(4,128)(2,1)} %reshape_reshape.23, ...), kind=kLoop, calls=%fused_computation.36 | loop fusion | flops 1032192 | bytes 1474576 | tf_op jit(solution)/shard_map/reduce_sum | solution.py:22
  34.1 0.7 pad_maximum_fusion.2
  34.8 1.6 %collective-permute-start = (bf16[256,384]{0,1:T(8,128)(2,1)}, bf16[256,384]{0,1:T(8,128)(2,1)}, u32[]{:S(2)}, u32[]{:S(2)}) collective-permute-start(bf16[256,384]{0,1:T(8,128)(2,1)} %pad_maximum_fusion.2), channel_id=1, source_target_pairs={{0,4},{4,0},{8,12},{12,8},{1,5},{5,1},{9,13},{13,9},{2,6},{6,2},{1... | collective-permute-start | bytes 589832 | tf_op jit(solution)/shard_map/ppermute | solution.py:16
  36.4 0.3 reshape_reshape.21
  37.4 22.0 %while.3 = (s32[]{:T(128)}, f32[2,512,4]{1,2,0:T(4,128)S(1)}, f32[2,512,4]{1,2,0:T(4,128)}, f32[2,512,4,48]{1,0,3,2:T(2,128)}, bf16[2,512,4,48]{1,3,2,0:T(8,128)...) while((s32[]{:T(128)}, f32[2,512,4]{1,2,0:T(4,128)S(1)}, ...), condition=%wide.region_3.4_spmd.clone, body=%wide.region_0.3_spmd.clone.sunk | while | flops 425717760 | bytes 36048076 | solution.py:56
  37.5 1.5 %fusion.67 = (f32[4,512]{1,0:T(4,128)S(1)}, f32[4,512,1024]{2,1,0:T(8,128)S(1)}) fusion(pred[1024]{0:T(1024)(128)(4,1)S(1)} %get-tuple-element.270, bf16[1024,4,48]{0,2,1:T(8,128)(2,1)S(1)} %get-tuple-element.268, bf16[2,512,4,48]{1,3,2,0:T(8,128)(2,1)S(1)} %get-tuple-element.267, s32[]{:T(128)S(6)} %copy.88), kind=kOutput, calls=%fused_computation.3.clone.1 | convolution fusion | flops 207616000 | bytes 8987652 | tf_op jit(solution)/shard_map/while/body/eval_jaxpr/qhd,khd->hqk/dot_general | solution.py:44
  38.9 2.1 %fusion.68 = f32[4,512]{1,0:T(4,128)S(1)} fusion(f32[4,512,1024]{2,1,0:T(8,128)S(1)} %get-tuple-element.239, f32[4,512]{1,0:T(4,128)S(1)} %get-tuple-element.240, pred[1024]{0:T(1024)(128)(4,1)S(1)} %get-tuple-element.270), kind=kLoop, calls=%fused_computation.5.clone.1 | loop fusion | flops 8386560 | bytes 8406016 | tf_op jit(solution)/shard_map/while/body/eval_jaxpr/reduce_sum | solution.py:50
  41.0 0.6 bitcast_dynamic-update-slice_fusion.3
  41.6 1.8 %fusion.69 = f32[1,512,4,48]{1,3,2,0:T(8,128)S(1)} fusion(bf16[1024,4,48]{0,2,1:T(8,128)(2,1)S(1)} %copy-done.9, f32[4,512,1024]{2,1,0:T(8,128)S(1)} %get-tuple-element.239, f32[4,512]{1,0:T(4,128)S(1)} %get-tuple-element.240, pred[1024]{0:T(1024)(128)(4,1)S(1)} %get-tuple-element.270), kind=kOutput, calls=%fused_computation.8.clone.1 | convolution fusion | flops 209715200 | bytes 9184256 | tf_op jit(solution)/shard_map/while/body/eval_jaxpr/hqk,khd->qhd/dot_general | solution.py:51
  43.5 0.4 copy.80
  43.9 3.6 %dynamic_update_slice.35 = f32[2,512,4,48]{1,0,3,2:T(2,128)S(1)} dynamic-update-slice(f32[2,512,4,48]{1,0,3,2:T(2,128)S(1)} %copy-done.6, f32[1,512,4,48]{1,0,3,2:T(1,128)S(1)} %copy.80, s32[]{:T(128)S(6)} %copy.88, s32[]{:T(128)} %constant.138.clone.1..sunk, s32[]{:T(128)} %constant.138.clone.1..sunk, s32[]{:T(128)} %constant.138.clone.1..sunk) | dynamic-update-slice | bytes 786436 | tf_op jit(solution)/shard_map/while/body/jit(dynamic_update_index_in_dim)/dynamic_update_slice | solution.py:56
  47.6 0.9 copy-done.7
  48.5 1.5 %fusion.67 = (f32[4,512]{1,0:T(4,128)S(1)}, f32[4,512,1024]{2,1,0:T(8,128)S(1)}) fusion(pred[1024]{0:T(1024)(128)(4,1)S(1)} %get-tuple-element.270, bf16[1024,4,48]{0,2,1:T(8,128)(2,1)S(1)} %get-tuple-element.268, bf16[2,512,4,48]{1,3,2,0:T(8,128)(2,1)S(1)} %get-tuple-element.267, s32[]{:T(128)S(6)} %copy.88), kind=kOutput, calls=%fused_computation.3.clone.1 | convolution fusion | flops 207616000 | bytes 8987652 | tf_op jit(solution)/shard_map/while/body/eval_jaxpr/qhd,khd->hqk/dot_general | solution.py:44
  50.0 2.1 %fusion.68 = f32[4,512]{1,0:T(4,128)S(1)} fusion(f32[4,512,1024]{2,1,0:T(8,128)S(1)} %get-tuple-element.239, f32[4,512]{1,0:T(4,128)S(1)} %get-tuple-element.240, pred[1024]{0:T(1024)(128)(4,1)S(1)} %get-tuple-element.270), kind=kLoop, calls=%fused_computation.5.clone.1 | loop fusion | flops 8386560 | bytes 8406016 | tf_op jit(solution)/shard_map/while/body/eval_jaxpr/reduce_sum | solution.py:50
  52.0 0.6 bitcast_dynamic-update-slice_fusion.3
  52.6 1.8 %fusion.69 = f32[1,512,4,48]{1,3,2,0:T(8,128)S(1)} fusion(bf16[1024,4,48]{0,2,1:T(8,128)(2,1)S(1)} %copy-done.9, f32[4,512,1024]{2,1,0:T(8,128)S(1)} %get-tuple-element.239, f32[4,512]{1,0:T(4,128)S(1)} %get-tuple-element.240, pred[1024]{0:T(1024)(128)(4,1)S(1)} %get-tuple-element.270), kind=kOutput, calls=%fused_computation.8.clone.1 | convolution fusion | flops 209715200 | bytes 9184256 | tf_op jit(solution)/shard_map/while/body/eval_jaxpr/hqk,khd->qhd/dot_general | solution.py:51
  54.5 0.4 copy.80
  54.9 3.6 %dynamic_update_slice.35 = f32[2,512,4,48]{1,0,3,2:T(2,128)S(1)} dynamic-update-slice(f32[2,512,4,48]{1,0,3,2:T(2,128)S(1)} %copy-done.6, f32[1,512,4,48]{1,0,3,2:T(1,128)S(1)} %copy.80, s32[]{:T(128)S(6)} %copy.88, s32[]{:T(128)} %constant.138.clone.1..sunk, s32[]{:T(128)} %constant.138.clone.1..sunk, s32[]{:T(128)} %constant.138.clone.1..sunk) | dynamic-update-slice | bytes 786436 | tf_op jit(solution)/shard_map/while/body/jit(dynamic_update_index_in_dim)/dynamic_update_slice | solution.py:56
  58.6 0.9 copy-done.7
  59.8 0.5 collective-permute-start.3
  60.3 6.2 %collective-permute-done.3 = bf16[64,384]{0,1:T(8,128)(2,1)S(1)} collective-permute-done((bf16[64,384]{0,1:T(8,128)(2,1)}, bf16[64,384]{0,1:T(8,128)(2,1)S(1)}, u32[]{:S(2)}, u32[]{:S(2)}) %collective-permute-start.3) | collective-permute-done | bytes 49184 | tf_op jit(solution)/shard_map/ppermute | solution.py:120
  66.6 0.7 copy.45
  67.3 2.2 %copy.70 = f32[24,8,2,512]{3,1,2,0:T(8,128)} copy(f32[24,8,2,512]{3,2,1,0:T(2,128)} %bitcast.129) | data formatting | bytes 1572864
  69.7 0.9 broadcast_in_dim.293
  70.6 2.2 %collective-permute-done.4 = bf16[64,384]{0,1:T(8,128)(2,1)S(1)} collective-permute-done((bf16[64,384]{0,1:T(8,128)(2,1)S(1)}, bf16[64,384]{0,1:T(8,128)(2,1)S(1)}, u32[]{:S(2)}, u32[]{:S(2)}) %collective-permute-start.4) | collective-permute-done | bytes 49184 | tf_op jit(solution)/shard_map/ppermute | solution.py:120
  72.9 1.2 concatenate.41
  74.3 0.2 fusion.50
  74.7 1.7 %pad_maximum_fusion.1 = bf16[512,384]{0,1:T(8,128)(2,1)} fusion(bf16[256,384]{0,1:T(8,128)(2,1)} %collective-permute-done, bf16[256,192]{0,1:T(8,128)(2,1)S(1)} %bitcast.124, bf16[256,192]{0,1:T(8,128)(2,1)S(1)} %bitcast.127), kind=kLoop, calls=%fused_computation.45 | loop fusion | flops 1179648 | bytes 786432 | tf_op jit(solution)/shard_map/concatenate | solution.py:94
  76.4 0.2 fusion.28
  76.7 0.8 copy.62
  77.5 1.2 broadcast_in_dim.317
  78.6 1.9 %broadcast_in_dim.318 = f32[1024,192]{1,0:T(8,128)} reshape(f32[64,16,4,48]{3,2,1,0:T(4,128)S(1)} %broadcast_in_dim.317) | data formatting | bytes 1572864 | tf_op jit(solution)/shard_map/jit(_where)/broadcast_in_dim | solution.py:32
  80.5 2.5 %copy.63 = f32[1024,192]{0,1:T(8,128)} copy(f32[1024,192]{1,0:T(8,128)} %broadcast_in_dim.318) | data formatting | bytes 1572864 | tf_op jit(solution)/shard_map/jit(_where)/broadcast_in_dim | solution.py:32
  83.1 0.7 broadcast_in_dim.323
  83.9 0.7 broadcast_in_dim.309
  84.6 9.2 %collective-permute-done.1 = bf16[512,384]{0,1:T(8,128)(2,1)} collective-permute-done((bf16[512,384]{0,1:T(8,128)(2,1)}, bf16[512,384]{0,1:T(8,128)(2,1)}, u32[]{:S(2)}, u32[]{:S(2)}) %collective-permute-start.1) | collective-permute-done | bytes 393248 | tf_op jit(solution)/shard_map/ppermute | solution.py:16
  93.9 1.1 pad_maximum_fusion
  95.1 0.8 fusion.17
  95.9 1.7 %fusion.18 = f32[4,256]{1,0:T(4,128)} fusion(f32[4,256,1024]{2,1,0:T(8,128)S(1)} %get-tuple-element.185, f32[4,256]{1,0:T(4,128)S(1)} %get-tuple-element.184, pred[4,1024]{1,0:T(4,128)(4,1)S(1)} %add_compare_fusion), kind=kLoop, calls=%fused_computation.20 | loop fusion | flops 4193280 | bytes 4206592 | tf_op jit(solution)/shard_map/while/body/eval_jaxpr/reduce_sum | solution.py:50
  97.6 1.2 fusion.25
  98.8 1.0 copy.60
  99.8 1.3 broadcast_in_dim.312
  101.1 1.9 %broadcast_in_dim.313 = f32[1024,192]{1,0:T(8,128)} reshape(f32[256,4,4,48]{3,2,1,0:T(4,128)S(1)} %broadcast_in_dim.312) | data formatting | bytes 1572864 | tf_op jit(solution)/shard_map/jit(_where)/broadcast_in_dim | solution.py:32
  103.0 1.7 %copy.61 = f32[1024,192]{0,1:T(8,128)S(1)} copy(f32[1024,192]{1,0:T(8,128)} %broadcast_in_dim.313) | data formatting | bytes 1572864 | tf_op jit(solution)/shard_map/jit(_where)/broadcast_in_dim | solution.py:32
  104.7 1.7 %broadcast_in_dim.319 = f32[256,4,4]{1,0,2:T(8,128)} broadcast(f32[256,4]{0,1:T(4,128)} %bitcast.137), dimensions={0,2} | broadcast | bytes 20480 | tf_op jit(solution)/shard_map/jit(_where)/broadcast_in_dim | solution.py:31
  106.3 1.9 %broadcast_in_dim.320 = f32[1024,4]{0,1:T(4,128)} reshape(f32[256,4,4]{1,0,2:T(8,128)} %broadcast_in_dim.319) | data formatting | bytes 32768 | tf_op jit(solution)/shard_map/jit(_where)/broadcast_in_dim | solution.py:31
  108.3 1.0 broadcast_in_dim.298
  109.3 1.9 %broadcast_in_dim.299 = f32[1024,4]{0,1:T(4,128)} reshape(f32[256,4,4]{1,0,2:T(8,128)} %broadcast_in_dim.298) | data formatting | bytes 32768 | tf_op jit(solution)/shard_map/jit(_where)/broadcast_in_dim | solution.py:30
  111.2 0.8 multiply_add_fusion
  112.1 1.1 fusion.29
  113.2 18.8 %all-gather.2.cloned.1.call-done = bf16[1024,768]{0,1:T(8,128)(2,1)} async-done(((bf16[1024,192]{0,1:T(8,128)(2,1)}), bf16[1024,768]{0,1:T(8,128)(2,1)}) %all-gather.2.cloned.1.call-update) | async-done | bytes 1572880 | tf_op jit(solution)/shard_map/all_gather | solution.py:149
  132.0 2.9 %fusion.23 = bf16[1024,192]{0,1:T(8,128)(2,1)} fusion(bf16[1024,768]{0,1:T(8,128)(2,1)} %all-gather.2.cloned.1.call-done, bf16[768,768]{1,0:T(8,128)(2,1)S(1)} %copy-done, s32[]{:T(128)S(6)} %select_n.159, pred[1024]{0:T(1024)(128)(4,1)S(1)} %get-tuple-element.280), kind=kOutput, calls=%fused_computation.25 | convolution fusion | flops 302383104 | bytes 2360324 | tf_op jit(solution)/shard_map/dot_general | solution.py:148
  (71 shorter events, 1.9 us)
Async XLA Ops:
  6.5 125.4 %copy-start = (bf16[768,768]{1,0:T(8,128)(2,1)S(1)}, bf16[768,768]{1,0:T(8,128)(2,1)}, u32[]{:S(2)}) copy-start(bf16[768,768]{1,0:T(8,128)(2,1)} %param.11) | copy-start | bytes 3538948
  6.5 6.3 %copy-start.8 = (bf16[1024,192]{0,1:T(8,128)(2,1)S(1)}, bf16[1024,192]{0,1:T(8,128)(2,1)}, u32[]{:S(2)}) copy-start(bf16[1024,192]{0,1:T(8,128)(2,1)} %param.10) | copy-start | bytes 1179652
  6.5 125.4 %all-gather.2.cloned.1.call-start = ((), (), s32[]{:S(2)}) async-start(), calls=%async_computation | async-start | bytes 1966080 | tf_op jit(solution)/shard_map/all_gather | solution.py:149
  10.1 17.6 %copy-start.12 = (s32[4]{0:T(128)}, s32[4]{0:T(128)S(1)}, u32[]{:S(2)}) copy-start(s32[4]{0:T(128)S(1)} %get-tuple-element.180) | copy-start | bytes 52
  20.0 39.8 %collective-permute-start.2 = (bf16[64,384]{0,1:T(8,128)(2,1)S(1)}, bf16[64,384]{0,1:T(8,128)(2,1)}, u32[]{:S(2)}, u32[]{:S(2)}) collective-permute-start(bf16[64,384]{0,1:T(8,128)(2,1)S(1)} %pad_maximum_fusion.3), channel_id=1, source_target_pairs={{0,4},{4,8},{8,12},{12,0},{1,5},{5,9},{9,13},{13,1},{2,6},{6,10},{... | collective-permute-start | bytes 147464 | tf_op jit(solution)/shard_map/ppermute | solution.py:120
  24.8 11.6 %copy-start.4 = (bf16[1024,192]{0,1:T(8,128)(2,1)S(1)}, bf16[1024,192]{0,1:T(8,128)(2,1)}, u32[]{:S(2)}) copy-start(bf16[1024,192]{0,1:T(8,128)(2,1)} %param.8) | copy-start | bytes 1179652
  26.3 11.2 %copy-start.1 = (bf16[1024,192]{0,1:T(8,128)(2,1)S(1)}, bf16[1024,192]{0,1:T(8,128)(2,1)}, u32[]{:S(2)}) copy-start(bf16[1024,192]{0,1:T(8,128)(2,1)} %param.9) | copy-start | bytes 1179652
  27.8 9.7 %copy-start.14 = (pred[4,4]{1,0:T(4,128)(4,1)}, pred[4,4]{1,0:T(4,128)(4,1)S(1)}, u32[]{:S(2)}) copy-start(pred[4,4]{1,0:T(4,128)(4,1)S(1)} %iota_compare_fusion.1) | copy-start | bytes 52
  34.8 39.9 %collective-permute-start = (bf16[256,384]{0,1:T(8,128)(2,1)}, bf16[256,384]{0,1:T(8,128)(2,1)}, u32[]{:S(2)}, u32[]{:S(2)}) collective-permute-start(bf16[256,384]{0,1:T(8,128)(2,1)} %pad_maximum_fusion.2), channel_id=1, source_target_pairs={{0,4},{4,0},{8,12},{12,8},{1,5},{5,1},{9,13},{13,9},{2,6},{6,2},{1... | collective-permute-start | bytes 589832 | tf_op jit(solution)/shard_map/ppermute | solution.py:16
  37.4 22.3 %copy-start.13 = (s32[4]{0:T(128)S(1)}, s32[4]{0:T(128)}, u32[]{:S(2)}) copy-start(s32[4]{0:T(128)} %copy-done.12) | copy-start | bytes 52
  38.9 2.7 %copy-start.9 = (bf16[1024,4,48]{0,2,1:T(8,128)(2,1)S(1)}, bf16[1024,4,48]{0,2,1:T(8,128)(2,1)}, u32[]{:S(2)}) copy-start(bf16[1024,4,48]{0,2,1:T(8,128)(2,1)} %get-tuple-element.269) | copy-start | bytes 1179652 | tf_op jit(solution)/shard_map/while
  41.6 2.3 %copy-start.6 = (f32[2,512,4,48]{1,0,3,2:T(2,128)S(1)}, f32[2,512,4,48]{1,0,3,2:T(2,128)}, u32[]{:S(2)}) copy-start(f32[2,512,4,48]{1,0,3,2:T(2,128)} %get-tuple-element.256) | copy-start | bytes 2359300 | tf_op jit(solution)/shard_map/while
  47.6 0.9 copy-start.7
  49.9 2.7 %copy-start.9 = (bf16[1024,4,48]{0,2,1:T(8,128)(2,1)S(1)}, bf16[1024,4,48]{0,2,1:T(8,128)(2,1)}, u32[]{:S(2)}) copy-start(bf16[1024,4,48]{0,2,1:T(8,128)(2,1)} %get-tuple-element.269) | copy-start | bytes 1179652 | tf_op jit(solution)/shard_map/while
  52.6 2.3 %copy-start.6 = (f32[2,512,4,48]{1,0,3,2:T(2,128)S(1)}, f32[2,512,4,48]{1,0,3,2:T(2,128)}, u32[]{:S(2)}) copy-start(f32[2,512,4,48]{1,0,3,2:T(2,128)} %get-tuple-element.256) | copy-start | bytes 2359300 | tf_op jit(solution)/shard_map/while
  58.6 0.9 copy-start.7
  59.5 10.0 %copy-start.11 = (f32[2,512,4]{1,2,0:T(4,128)}, f32[2,512,4]{1,2,0:T(4,128)S(1)}, u32[]{:S(2)}) copy-start(f32[2,512,4]{1,2,0:T(4,128)S(1)} %get-tuple-element.87) | copy-start | bytes 49156
  59.8 6.7 %collective-permute-start.3 = (bf16[64,384]{0,1:T(8,128)(2,1)}, bf16[64,384]{0,1:T(8,128)(2,1)S(1)}, u32[]{:S(2)}, u32[]{:S(2)}) collective-permute-start(bf16[64,384]{0,1:T(8,128)(2,1)} %collective-permute-done.2), channel_id=1, source_target_pairs={{0,4},{4,8},{8,12},{12,0},{1,5},{5,9},{9,13},{13,1},{2,6},{6,10},{... | collective-permute-start | bytes 147464 | tf_op jit(solution)/shard_map/ppermute | solution.py:120
  66.5 6.4 %collective-permute-start.4 = (bf16[64,384]{0,1:T(8,128)(2,1)S(1)}, bf16[64,384]{0,1:T(8,128)(2,1)S(1)}, u32[]{:S(2)}, u32[]{:S(2)}) collective-permute-start(bf16[64,384]{0,1:T(8,128)(2,1)S(1)} %collective-permute-done.3), channel_id=1, source_target_pairs={{0,4},{4,8},{8,12},{12,0},{1,5},{5,9},{9,13},{13,1},{2,6},{6,10},{... | collective-permute-start | bytes 147464 | tf_op jit(solution)/shard_map/ppermute | solution.py:120
  76.4 17.4 %collective-permute-start.1 = (bf16[512,384]{0,1:T(8,128)(2,1)}, bf16[512,384]{0,1:T(8,128)(2,1)}, u32[]{:S(2)}, u32[]{:S(2)}) collective-permute-start(bf16[512,384]{0,1:T(8,128)(2,1)} %pad_maximum_fusion.1), channel_id=1, source_target_pairs={{0,8},{4,12},{8,0},{12,4},{1,9},{5,13},{9,1},{13,5},{2,10},{6,14},... | collective-permute-start | bytes 1179656 | tf_op jit(solution)/shard_map/ppermute | solution.py:16
  80.5 14.5 %copy-start.5 = (bf16[256,4,48]{2,1,0:T(4,128)(2,1)S(1)}, bf16[256,4,48]{2,1,0:T(4,128)(2,1)}, u32[]{:S(2)}) copy-start(bf16[256,4,48]{2,1,0:T(4,128)(2,1)} %get-tuple-element.146) | copy-start | bytes 294916
  101.1 10.1 %copy-start.10 = (pred[1024,4]{0,1:T(4,128)(4,1)S(1)}, pred[1024,4]{0,1:T(4,128)(4,1)}, u32[]{:S(2)}) copy-start(pred[1024,4]{0,1:T(4,128)(4,1)} %broadcast_in_dim.293) | copy-start | bytes 12292
  103.0 9.1 %copy-start.2 = (f32[1024,192]{0,1:T(8,128)S(1)}, f32[1024,192]{0,1:T(8,128)}, u32[]{:S(2)}) copy-start(f32[1024,192]{0,1:T(8,128)} %copy.63) | copy-start | bytes 2359300
  103.0 9.1 %copy-start.3 = (f32[24,8,2,512]{3,1,2,0:T(8,128)S(1)}, f32[24,8,2,512]{3,1,2,0:T(8,128)}, u32[]{:S(2)}) copy-start(f32[24,8,2,512]{3,1,2,0:T(8,128)} %copy.70) | copy-start | bytes 2359300
Sparse Core Ops, SparseCore 0:
  113.3 18.6 all-gather.1
